TPU v7x, 16 devices: a 4x2x1 block of a 4x4x8 slice. The times are simulated.
16 devices in a mesh: dp: 2 (over y, z), ep: 8 (over x, core).
Axes of the slice: x: 4, y: 2, z: 1, core: 2. Of those that a mesh axis runs over, the one named last changes fastest.
The devices are a block of a 4x4x8 slice.
Arguments:
- x_in: bfloat16 [1024, 2880], P(('dp', 'ep')), parts along dimension 0
- expert_ids: int32 [1024, 4], P(('dp', 'ep')), parts along dimension 0
- norm_weight: bfloat16 [2880], replicated
- router_w: bfloat16 [2880, 32], replicated
- router_b: bfloat16 [32], replicated
- w_gate_up: bfloat16 [32, 2880, 5760], P('ep')
- b_gate_up: bfloat16 [32, 5760], P('ep')
- w_down: bfloat16 [32, 2880, 2880], P('ep')
- b_down: bfloat16 [32, 2880], P('ep')
Outputs:
- output: bfloat16 [1024, 2880], P(('dp', 'ep')), parts along dimension 0
There are 2 independent parts. A program takes and returns all parts, laid end to end along the dimension named above; an argument that names none is the same for every part.
All inputs are finite; a program needn't handle non-finite values.
Results may differ from a plain program's by a relative error of at most 0.00686295.
Values are sent between devices in bfloat16 or wider.
A program may use at most 768 MiB of HBM per device.

v0:
```python
import jax
import jax.numpy as jnp
from jax import lax
from jax.sharding import PartitionSpec as P

CAPACITY_FACTOR = 4
EPSILON = 1e-5
LIMIT = 7.0
ALPHA = 1.702


def rms_norm(x_in, norm_weight):
    x_float = x_in.astype(jnp.float32)
    inv_rms = lax.rsqrt(jnp.mean(x_float * x_float, axis=-1, keepdims=True) + EPSILON)
    return (x_float * inv_rms * norm_weight.astype(jnp.float32)).astype(jnp.bfloat16)


def route_gates(hidden, expert_ids, router_w, router_b):
    logits = jnp.dot(hidden, router_w, preferred_element_type=jnp.float32) + router_b.astype(jnp.float32)
    return jax.nn.softmax(jnp.take_along_axis(logits, expert_ids, axis=1), axis=-1)


def clamped_glu(gate_up):
    gate = jnp.minimum(gate_up[..., 0::2].astype(jnp.float32), LIMIT)
    linear = jnp.clip(gate_up[..., 1::2].astype(jnp.float32), -LIMIT, LIMIT)
    return (gate * jax.nn.sigmoid(ALPHA * gate) * (linear + 1.0)).astype(jnp.bfloat16)


def slot_tables(flat_ids, experts, capacity):
    pairs = flat_ids.shape[0]
    onehot = (flat_ids[:, None] == jnp.arange(experts, dtype=jnp.int32)[None, :]).astype(jnp.int32)
    rank = jnp.sum((jnp.cumsum(onehot, axis=0) - 1) * onehot, axis=1)
    slot_pair = jnp.zeros((experts * capacity,), jnp.int32).at[flat_ids * capacity + rank].set(jnp.arange(pairs, dtype=jnp.int32))
    return slot_pair, rank, jnp.sum(onehot, axis=0)


def mix_residual(x_in, gates, picked):
    mixed = jnp.sum(gates[:, :, None] * picked.astype(jnp.float32), axis=1)
    return (x_in.astype(jnp.float32) + mixed).astype(jnp.bfloat16)


def solution(mesh):
    n_group = mesh.shape['ep']
    rows_spec = P(('dp', 'ep'), None)

    def local_block(x_in, expert_ids, norm_weight, router_w, router_b, w_gate_up, b_gate_up, w_down, b_down):
        tok_dev, d_model = x_in.shape
        top_k = expert_ids.shape[1]
        local_exp = w_gate_up.shape[0]
        experts = local_exp * n_group
        capacity = CAPACITY_FACTOR * top_k * tok_dev // experts
        hidden = rms_norm(x_in, norm_weight)
        gates = route_gates(hidden, expert_ids, router_w, router_b)
        flat_ids = expert_ids.reshape(-1)
        slot_pair, rank, _ = slot_tables(flat_ids, experts, capacity)
        rows = jnp.take(hidden, slot_pair // top_k, axis=0).reshape(n_group, local_exp, capacity, d_model)
        received = lax.all_to_all(rows, 'ep', 0, 0, tiled=True)
        gate_up = (jnp.einsum('sgcd,gdf->gscf', received, w_gate_up, preferred_element_type=jnp.float32) + b_gate_up[:, None, None, :].astype(jnp.float32)).astype(jnp.bfloat16)
        expert_out = (jnp.einsum('gscf,gfd->gscd', clamped_glu(gate_up), w_down, preferred_element_type=jnp.float32) + b_down[:, None, None, :].astype(jnp.float32)).astype(jnp.bfloat16)
        returned = lax.all_to_all(expert_out, 'ep', 1, 1, tiled=True)
        back_slot = ((flat_ids % local_exp) * n_group + flat_ids // local_exp) * capacity + rank
        picked = jnp.take(returned.reshape(-1, d_model), back_slot, axis=0).reshape(tok_dev, top_k, d_model)
        return mix_residual(x_in, gates, picked)

    return jax.shard_map(local_block, mesh=mesh, in_specs=(rows_spec, rows_spec, P(), P(), P(), P('ep', None, None), P('ep', None), P('ep', None, None), P('ep', None)), out_specs=rows_spec, check_vma=False)
```

profile of v0, /device:TPU:112, one launch (start us, length us, event | category | flops | bytes accessed | tf_op | source)
XLA Modules:
  0.0 699.9 jit_solution(16142788390908179631)
XLA Ops:
  0.0 0.8 copy.25
  0.8 0.1 eq.28
  0.9 0.1 reshape.243
  1.0 0.1 reshape.245
  1.1 0.6 reduce-window.6
  1.7 0.2 slice_reduce_fusion
  2.1 0.6 compare_select_fusion.3
  2.7 1.4 scatter_custom_fusion
  4.1 1.2 fusion.13
  5.3 0.7 convert_element_type.48
  6.1 1.1 fusion.15
  7.3 6.6 gather_fusion
  13.9 6.0 broadcast_select_fusion
  19.8 5.4 all-to-all-start
  25.3 69.3 %all-to-all-done = bf16[8,4,32,2880]{3,2,1,0:T(8,128)(2,1)} async-done(((bf16[8,4,32,2880]{3,2,1,0:T(8,128)(2,1)}), bf16[8,4,32,2880]{3,2,1,0:T(8,128)(2,1)}, u32[]{:S(2)}, u32[]{:S(2)}) %all-to-all-start) | async-done | bytes 5898272 | tf_op jit(solution)/shard_map/all_to_all | solution.py:57
  94.6 56.0 %add_convert_fusion = bf16[4,8,32,5760]{3,2,1,0:T(8,128)(2,1)} fusion(bf16[4,2880,5760]{2,1,0:T(8,128)(2,1)} %param.14, f32[4,5760]{1,0:T(4,128)S(1)} %convert_element_type.52, bf16[8,4,32,2880]{3,2,1,0:T(8,128)(2,1)} %all-to-all-done), kind=kOutput, calls=%fused_computation.8 | convolution fusion | flops 33985658880 | bytes 150497280 | tf_op jit(solution)/shard_map/sgcd,gdf->gscf/dot_general | solution.py:58
  150.6 214.9 %slice.15 = bf16[4,8,32,2880]{3,2,1,0:T(8,128)(2,1)} slice(bf16[4,8,32,5760]{3,2,1,0:T(8,128)(2,1)} %add_convert_fusion), slice={[0:4:1], [0:8:1], [0:32:1], [1:5760:2]} | slice | bytes 11796480 | tf_op jit(solution)/shard_map/slice | solution.py:25
  365.5 200.9 %slice.14 = bf16[4,8,32,2880]{3,2,1,0:T(8,128)(2,1)} slice(bf16[4,8,32,5760]{3,2,1,0:T(8,128)(2,1)} %add_convert_fusion), slice={[0:4:1], [0:8:1], [0:32:1], [0:5760:2]} | slice | bytes 11796480 | tf_op jit(solution)/shard_map/slice | solution.py:24
  566.4 35.6 %add_convert_fusion.1 = bf16[4,8,32,2880]{3,2,1,0:T(8,128)(2,1)} fusion(f32[4,2880]{1,0:T(4,128)S(1)} %convert_element_type.57, bf16[4,2880,2880]{2,1,0:T(8,128)(2,1)} %param.16, bf16[4,8,32,2880]{3,2,1,0:T(8,128)(2,1)} %slice.15, bf16[4,8,32,2880]{3,2,1,0:T(8,128)(2,1)} %slice.14), kind=kOutput, calls=%fused_computation.9 | convolution fusion | flops 17028218880 | bytes 84096000 | tf_op jit(solution)/shard_map/gscf,gfd->gscd/dot_general | solution.py:59
  602.0 5.9 copy.37
  607.9 5.0 all-to-all-start.1
  613.3 0.1 reshape.263
  613.4 0.2 convolution_add_fusion
  613.6 2.0 gather_fusion.2
  615.8 0.1 fusion.40
  615.9 0.2 fusion.29
  616.3 65.8 %all-to-all-done.1 = bf16[4,8,32,2880]{3,2,0,1:T(8,128)(2,1)} async-done(((bf16[4,8,32,2880]{3,2,0,1:T(8,128)(2,1)}), bf16[4,8,32,2880]{3,2,0,1:T(8,128)(2,1)}, u32[]{:S(2)}, u32[]{:S(2)}) %all-to-all-start.1) | async-done | bytes 5898272 | tf_op jit(solution)/shard_map/all_to_all | solution.py:60
  682.1 5.9 copy.38
  688.0 6.6 gather_fusion.1
  694.6 0.4 gather.20
  695.0 3.0 multiply_reduce_fusion
  698.0 1.8 fusion.16
  (44 shorter events, 0.8 us)
Async XLA Ops:
  0.0 613.4 %copy-start = (bf16[2880,32]{0,1:T(8,128)(2,1)S(1)}, bf16[2880,32]{0,1:T(8,128)(2,1)}, u32[]{:S(2)}) copy-start(bf16[2880,32]{0,1:T(8,128)(2,1)} %param.12) | copy-start | bytes 552964
  0.8 5.2 copy-start.3
  2.1 0.6 copy-start.7
  7.3 6.6 copy-start.1
  19.8 5.4 copy-start.6
  19.8 5.5 copy-start.5
  19.8 74.8 %all-to-all-start = ((bf16[8,4,32,2880]{3,2,1,0:T(8,128)(2,1)}), bf16[8,4,32,2880]{3,2,1,0:T(8,128)(2,1)}, u32[]{:S(2)}, u32[]{:S(2)}) async-start(bf16[8,4,32,2880]{3,2,1,0:T(8,128)(2,1)} %broadcast_select_fusion), calls=%async_computation | async-start | bytes 12058624 | tf_op jit(solution)/shard_map/all_to_all | solution.py:57
  607.9 5.1 copy-start.8
  607.9 5.2 copy-start.11
  607.9 5.2 copy-start.9
  607.9 5.3 copy-start.4
  607.9 5.5 copy-start.2
  607.9 74.1 %all-to-all-start.1 = ((bf16[4,8,32,2880]{3,2,0,1:T(8,128)(2,1)}), bf16[4,8,32,2880]{3,2,0,1:T(8,128)(2,1)}, u32[]{:S(2)}, u32[]{:S(2)}) async-start(bf16[4,8,32,2880]{3,2,0,1:T(8,128)(2,1)} %copy.37), calls=%async_computation.1 | async-start | bytes 12058624 | tf_op jit(solution)/shard_map/all_to_all | solution.py:60
  613.6 2.1 copy-start.10
where the time goes:
time: 701 us; the launch traced here: 700 us
  local copies, waits for them, and re-layouts  447 us (64%)
  waiting for transfers between devices  135 us (19%)
  matrix products  91.8 us (13%)
  other arithmetic  15.7 us (2%)
  starting transfers between devices  10.5 us (1%)
    slice x1, local copies, waits for them, and re-layouts, clamped_glu(): linear = jnp.clip(gate_up[..., 1::2].astype(jnp.float32), -LIMIT, LIMIT)  215 us
    slice x1, local copies, waits for them, and re-layouts, clamped_glu(): gate = jnp.minimum(gate_up[..., 0::2].astype(jnp.float32), LIMIT)  201 us
    all_to_all x1, waiting for transfers between devices, local_block(): received = lax.all_to_all(rows, 'ep', 0, 0, tiled=True)  69.3 us
    all_to_all x1, waiting for transfers between devices, local_block(): returned = lax.all_to_all(expert_out, 'ep', 1, 1, tiled=True)  65.8 us
    dot_general x1, matrix products, local_block(): jnp.einsum('sgcd,gdf->gscf', received, w_gate_up, preferred_element_type=...  56 us
    dot_general x1, matrix products, local_block(): jnp.einsum('gscf,gfd->gscd', clamped_glu(gate_up), w_down, preferred_elem...  35.6 us
  transfers between devices with their start and end apart: 2, of which 2 were waited for; matrix products, arithmetic and copies ran while one was open for 0% of the time, Pallas kernels for 0%

commit v1 on v0

v1 whole, which is shorter than its diff:
```python
import functools

import jax
import jax.numpy as jnp
from jax import lax
from jax.experimental import pallas as pl
from jax.experimental.pallas import tpu as pltpu
from jax.sharding import PartitionSpec as P

EPSILON = 1e-5
LIMIT = 7.0
ALPHA = 1.702
F32 = jnp.float32
BF16 = jnp.bfloat16
VMEM_LIMIT = 63 * 1024 * 1024


def dot32(a, b):
    return jnp.dot(a, b, preferred_element_type=F32)


def dot_t(a, b):
    return lax.dot_general(a, b, (((0,), (0,)), ((), ())), preferred_element_type=F32)


def dispatch_kernel(n, local_exp, x_ref, ids_ref, g_ref, wr_ref, br_ref, hall, pos_ref, post_ref, p_ref,
                    mall, sa, ra, sb, rb, sc, rc, sd, rd, sm, rm):
    me = lax.axis_index('ep')
    chips = n // 2
    chip, core = me // 2, me % 2
    partner = chip * 2 + (1 - core)
    right_chip, left_chip = (chip + 1) % chips, (chip + chips - 1) % chips
    far_chip = (chip + 2) % chips
    right, left = right_chip * 2 + core, left_chip * 2 + core
    far = far_chip * 2 + core
    tok, _ = x_ref.shape
    top_k = ids_ref.shape[1]
    experts = wr_ref.shape[1]
    half = tok // 2

    barrier = pltpu.get_barrier_semaphore()
    for k in range(1, n):
        pl.semaphore_signal(barrier, inc=1, device_id={'ep': (me + k) % n}, device_id_type=pl.DeviceIdType.MESH)

    x = x_ref[...].astype(F32)
    inv = lax.rsqrt(jnp.mean(x * x, axis=-1, keepdims=True) + EPSILON)
    h = (x * inv * g_ref[...].astype(F32)).astype(BF16)
    hall[me] = h
    logits = dot32(h, wr_ref[...]) + br_ref[...].astype(F32)
    lane = lax.broadcasted_iota(jnp.int32, (tok, experts), 1)
    hot = [ids_ref[:, k:k + 1] == lane for k in range(top_k)]
    picked = [jnp.sum(jnp.where(hk, logits, 0.0), axis=1, keepdims=True) for hk in hot]
    top = functools.reduce(jnp.maximum, picked)
    ex = [jnp.exp(v - top) for v in picked]
    total = functools.reduce(jnp.add, ex)
    gates = jnp.zeros((tok, experts), F32)
    chosen = jnp.zeros((tok, experts), F32)
    for k in range(top_k):
        gates = gates + jnp.where(hot[k], ex[k] / total, 0.0)
        chosen = chosen + jnp.where(hot[k], 1.0, 0.0)
    mall[me, 0] = gates
    mall[me, 1] = chosen

    pl.semaphore_wait(barrier, n - 1)

    def copy(src, dst, ssem, rsem, dev):
        return pltpu.make_async_remote_copy(src_ref=src, dst_ref=dst, send_sem=ssem, recv_sem=rsem,
                                            device_id={'ep': dev}, device_id_type=pl.DeviceIdType.MESH)

    lo, hi = pl.ds(0, half), pl.ds(half, half)
    sends = []

    def start(c):
        c.start()
        sends.append(c)

    for i, (dev, parts) in enumerate(((right, (lo, hi)), (left, (hi, lo)))):
        for j, rows in enumerate(parts):
            start(copy(hall.at[me, rows], hall.at[me, rows], sb.at[i, j], rb.at[i, j], dev))
    start(copy(hall.at[me], hall.at[me], sa, ra, partner))
    metas = []
    for k in range(1, n):
        c = copy(mall.at[me], mall.at[me], sm.at[k - 1], rm.at[k - 1], (me + k) % n)
        c.start()
        metas.append(c)
    order = ((0, left, right, (lo, hi)), (1, right, left, (hi, lo)))
    for i, origin, onward, parts in order:
        slot = hall.at[origin, parts[0]]
        copy(slot, slot, sb.at[i, 0], rb.at[i, 0], origin).wait_recv()
        start(copy(slot, slot, sc.at[i], rc.at[i], onward))
        start(copy(slot, slot, sd.at[i, 0], rd.at[i, 0], partner))
    for i, origin, onward, parts in order:
        slot = hall.at[origin, parts[1]]
        copy(slot, slot, sb.at[i, 1], rb.at[i, 1], origin).wait_recv()
        start(copy(slot, slot, sd.at[i, 1], rd.at[i, 1], partner))
    for i, origin, onward, parts in order:
        slot = hall.at[far, parts[0]]
        copy(slot, slot, sc.at[i], rc.at[i], origin).wait_recv()
        start(copy(slot, slot, sd.at[i, 2], rd.at[i, 2], partner))

    for k in range(1, n):
        src = (me + n - k) % n
        copy(mall.at[src], mall.at[src], sm.at[k - 1], rm.at[k - 1], src).wait_recv()
    tokens = n * tok
    e0 = me * local_exp
    gates_all = mall[:, 0].reshape(tokens, experts)
    chosen_all = mall[:, 1].reshape(tokens, experts)
    lane_all = lax.broadcasted_iota(jnp.int32, (tokens, experts), 1)
    pick = (lax.broadcasted_iota(jnp.int32, (experts, 8), 0)
            == lax.broadcasted_iota(jnp.int32, (experts, 8), 1) + e0)
    pick = jnp.where(pick & (lax.broadcasted_iota(jnp.int32, (experts, 8), 1) < local_exp), 1.0, 0.0).astype(BF16)
    mine = dot32(chosen_all.astype(BF16), pick).astype(BF16)
    row = lax.broadcasted_iota(jnp.int32, (tokens, tokens), 0)
    col = lax.broadcasted_iota(jnp.int32, (tokens, tokens), 1)
    lower = jnp.where(col < row, 1.0, 0.0).astype(BF16)
    upper = jnp.where(row < col, 1.0, 0.0).astype(BF16)
    eye = jnp.where(row == col, 1.0, 0.0).astype(BF16)
    pos_ref[...] = jnp.where(mine.astype(F32) > 0.5, dot32(lower, mine), -1.0)
    post_ref[...] = jnp.where(dot_t(mine, eye) > 0.5, dot_t(mine, upper), -1.0)
    for e in range(local_exp):
        p_ref[:, e:e + 1] = jnp.sum(jnp.where(lane_all == e0 + e, gates_all, 0.0), axis=1, keepdims=True)

    copy(hall.at[partner], hall.at[partner], sa, ra, partner).wait_recv()
    for i, origin_chip, parts in ((0, left_chip, (lo, hi)), (1, right_chip, (hi, lo))):
        other = origin_chip * 2 + (1 - core)
        for j in range(2):
            slot = hall.at[other, parts[j]]
            copy(slot, slot, sd.at[i, j], rd.at[i, j], partner).wait_recv()
        slot = hall.at[far_chip * 2 + (1 - core), parts[0]]
        copy(slot, slot, sd.at[i, 2], rd.at[i, 2], partner).wait_recv()
    for c in sends:
        c.wait_send()
    for c in metas:
        c.wait_send()


def dispatch(x, ids, g, wr, br, n, local_exp):
    tok, d_model = x.shape
    tokens = n * tok
    vm = pl.BlockSpec(memory_space=pltpu.VMEM)
    dma = pltpu.SemaphoreType.DMA
    hall, pos, post, p = pl.pallas_call(
        functools.partial(dispatch_kernel, n, local_exp),
        out_shape=(jax.ShapeDtypeStruct((n, tok, d_model), BF16),
                   jax.ShapeDtypeStruct((tokens, 8), F32),
                   jax.ShapeDtypeStruct((8, tokens), F32),
                   jax.ShapeDtypeStruct((tokens, local_exp), F32)),
        in_specs=[vm] * 5,
        out_specs=(vm,) * 4,
        scratch_shapes=[pltpu.VMEM((n, 2, tok, wr.shape[1]), F32),
                        dma, dma, dma((2, 2)), dma((2, 2)), dma((2,)), dma((2,)), dma((2, 3)), dma((2, 3)),
                        dma((n - 1,)), dma((n - 1,))],
        compiler_params=pltpu.CompilerParams(collective_id=0, has_side_effects=True, vmem_limit_bytes=VMEM_LIMIT),
        name='dispatch',
    )(x, ids, g, wr, br)
    return hall.reshape(tokens, d_model), pos, post, p


def gate_up_kernel(blk, m_blk, slots, hall, post_ref, w_hbm, b_ref, z_ref, wbuf, xg, perm, sems):
    local_exp, d_model, width = w_hbm.shape
    full, rest = width // blk, width % blk
    per_exp = full + (1 if rest else 0)
    total = local_exp * per_exp
    tokens = hall.shape[0]
    depth = slots - 1

    src = lax.broadcasted_iota(jnp.int32, (256, 256), 0)
    dst = lax.broadcasted_iota(jnp.int32, (256, 256), 1)
    want = jnp.where(dst < 128, 2 * dst, 2 * (dst - 128) + 1)
    perm[...] = jnp.where(src == want, 1.0, 0.0).astype(BF16)

    def block_copy(q, is_rest):
        e, j = q // per_exp, q % per_exp
        slot = q % slots
        if is_rest:
            return pltpu.make_async_copy(w_hbm.at[e, :, pl.ds(full * blk, rest)],
                                         wbuf.at[slot, :, pl.ds(0, rest)], sems.at[slot])
        return pltpu.make_async_copy(w_hbm.at[e, :, pl.ds(pl.multiple_of(j * blk, 128), blk)], wbuf.at[slot], sems.at[slot])

    def start(q):
        if not rest:
            block_copy(q, False).start()
            return
        j = lax.rem(q, per_exp)

        @pl.when(j < full)
        def _():
            block_copy(q, False).start()

        @pl.when(j == full)
        def _():
            block_copy(q, True).start()

    for q in range(depth):
        start(jnp.int32(q))

    def one_expert(e, carry):
        where_row = post_ref[pl.ds(e, 1), :]
        count = jnp.sum(jnp.where(where_row >= 0.0, 1.0, 0.0)).astype(jnp.int32)
        chunks = (count + (m_blk - 1)) // m_blk

        def gather(m, c):
            at = lax.broadcasted_iota(jnp.int32, (m_blk, tokens), 0) + m * m_blk
            onehot = jnp.where(at.astype(F32) == where_row, 1.0, 0.0).astype(BF16)
            xg[pl.ds(pl.multiple_of(m * m_blk, m_blk), m_blk), :] = dot32(onehot, hall[...]).astype(BF16)
            return c

        lax.fori_loop(0, chunks, gather, 0)

        def block(j, cols):
            q = e * per_exp + j
            slot = lax.rem(q, slots)

            @pl.when(q + depth < total)
            def _():
                start(q + depth)

            block_copy(q, cols != blk).wait()
            off = pl.multiple_of(j * blk, 128)
            bias = b_ref[e, :, pl.ds(off, cols)].astype(F32)

            def rows(m, c):
                at = pl.ds(pl.multiple_of(m * m_blk, m_blk), m_blk)
                u = (dot32(xg[at, :], wbuf[slot, :, :cols]) + bias).astype(BF16)
                for t in range(0, cols, 256):
                    wide = min(256, cols - t)
                    if wide == 256:
                        pm = perm[...]
                    else:
                        pm = jnp.concatenate([perm[:128, :64], perm[:128, 128:192]], axis=1)
                    al = dot32(u[:, t:t + wide], pm)
                    gate = jnp.minimum(al[:, :wide // 2], LIMIT)
                    linear = jnp.clip(al[:, wide // 2:], -LIMIT, LIMIT)
                    z = gate * jax.nn.sigmoid(ALPHA * gate) * (linear + 1.0)
                    zoff = pl.multiple_of(j * (blk // 2), 128) + t // 2
                    z_ref[e, at, pl.ds(zoff, wide // 2)] = z.astype(BF16)
                return c

            lax.fori_loop(0, chunks, rows, 0)

        def body(j, c):
            block(j, blk)
            return c

        lax.fori_loop(0, full, body, 0)
        if rest:
            block(jnp.int32(full), rest)
        return carry

    lax.fori_loop(0, local_exp, one_expert, 0)


def gate_up(hall, post, w, b, max_rows, blk, m_blk, slots):
    local_exp, d_model, width = w.shape
    vm = pl.BlockSpec(memory_space=pltpu.VMEM)
    return pl.pallas_call(
        functools.partial(gate_up_kernel, blk, m_blk, slots),
        out_shape=jax.ShapeDtypeStruct((local_exp, max_rows, width // 2), BF16),
        in_specs=[vm, vm, pl.BlockSpec(memory_space=pl.ANY), vm],
        out_specs=vm,
        scratch_shapes=[pltpu.VMEM((slots, d_model, blk), BF16), pltpu.VMEM((max_rows, d_model), BF16),
                        pltpu.VMEM((256, 256), BF16), pltpu.SemaphoreType.DMA((slots,))],
        compiler_params=pltpu.CompilerParams(vmem_limit_bytes=VMEM_LIMIT),
        name='gate_up',
    )(hall, post, w, b.reshape(local_exp, 1, width))


def down_kernel(blk, slots, z_ref, pos_ref, p_ref, w_hbm, b_ref, out_ref, wbuf, wrest, scat, sems, rsems):
    local_exp, d_ff, width = w_hbm.shape
    tokens = pos_ref.shape[0]
    max_rows = z_ref.shape[1]
    chunks = [(c, min(blk, width - c)) for c in range(0, width, blk)]
    total = len(chunks) * local_exp
    depth = slots - 1

    def block_copy(q):
        off, cols = chunks[q // local_exp]
        src = w_hbm.at[q % local_exp, :, pl.ds(off, cols)]
        if cols == blk:
            return pltpu.make_async_copy(src, wbuf.at[q % slots], sems.at[q % slots])
        return pltpu.make_async_copy(src, wrest.at[q % local_exp], rsems.at[q % local_exp])

    for q in range(depth):
        block_copy(q).start()
    slot_ids = lax.broadcasted_iota(jnp.int32, (tokens, max_rows), 1).astype(F32)
    for e in range(local_exp):
        scat[e] = jnp.where(pos_ref[:, e:e + 1] == slot_ids, 1.0, 0.0).astype(BF16)
    row_ids = lax.broadcasted_iota(jnp.int32, (max_rows, 1), 0).astype(F32)
    for c, (off, cols) in enumerate(chunks):
        for e in range(local_exp):
            q = c * local_exp + e
            if q + depth < total:
                block_copy(q + depth).start()
            block_copy(q).wait()
            count = jnp.max(pos_ref[:, e:e + 1]) + 1.0
            wv = wbuf[q % slots] if cols == blk else wrest[e]
            y = dot32(z_ref[e], wv) + b_ref[e, :, off:off + cols].astype(F32)
            y = jnp.where(row_ids < count, y, 0.0).astype(BF16)
            part = p_ref[:, e:e + 1] * dot32(scat[e], y)
            if e == 0:
                out_ref[:, off:off + cols] = part
            else:
                out_ref[:, off:off + cols] += part


def down(z, pos, p, w, b, blk, slots):
    local_exp, d_ff, width = w.shape
    tokens = pos.shape[0]
    vm = pl.BlockSpec(memory_space=pltpu.VMEM)
    return pl.pallas_call(
        functools.partial(down_kernel, blk, slots),
        out_shape=jax.ShapeDtypeStruct((tokens, width), F32),
        in_specs=[vm, vm, vm, pl.BlockSpec(memory_space=pl.ANY), vm],
        out_specs=vm,
        scratch_shapes=[pltpu.VMEM((slots, d_ff, blk), BF16), pltpu.VMEM((local_exp, d_ff, width % blk), BF16),
                        pltpu.VMEM((local_exp, tokens, z.shape[1]), BF16),
                        pltpu.SemaphoreType.DMA((slots,)), pltpu.SemaphoreType.DMA((local_exp,))],
        compiler_params=pltpu.CompilerParams(vmem_limit_bytes=VMEM_LIMIT),
        name='down',
    )(z, pos, p, w, b.reshape(local_exp, 1, width))


def solution(mesh):
    n = mesh.shape['ep']
    rows_spec = P(('dp', 'ep'), None)

    def local_block(x_in, expert_ids, norm_weight, router_w, router_b, w_gate_up, b_gate_up, w_down, b_down):
        tok, d_model = x_in.shape
        top_k = expert_ids.shape[1]
        local_exp = w_gate_up.shape[0]
        experts = local_exp * n
        max_rows = n * (4 * top_k * tok // experts)
        blk = 768 if w_gate_up.shape[2] >= 2048 else 256
        hall, pos, post, p = dispatch(x_in, expert_ids, norm_weight.reshape(1, -1), router_w, router_b.reshape(1, -1), n, local_exp)
        z = gate_up(hall, post, w_gate_up, b_gate_up, max_rows, blk, min(128, max_rows), 4)
        part = down(z, pos, p, w_down, b_down, blk, 4)
        mixed = lax.psum_scatter(part, 'ep', scatter_dimension=0, tiled=True)
        return (x_in.astype(F32) + mixed).astype(BF16)

    return jax.shard_map(local_block, mesh=mesh, in_specs=(rows_spec, rows_spec, P(), P(), P(), P('ep', None, None), P('ep', None), P('ep', None, None), P('ep', None)), out_specs=rows_spec, check_vma=False)
```

time: 701 us -> 182 us (0.26)
  local copies, waits for them, and re-layouts: 447 us -> 7.64 us
  Pallas kernels: 0 us -> 119 us
  waiting for transfers between devices: 135 us -> 39.2 us
  matrix products: 91.8 us -> 0 us
  other arithmetic: 15.7 us -> 1.93 us
  between operations: 0.29 us -> 13.5 us
  starting transfers between devices: 10.5 us -> 0.01 us
    slice x3 -> x0, local copies, waits for them, and re-layouts: 416 us -> none  [the longest x1 215 us: clamped_glu(): linear = jnp.clip(gate_up[..., 1::2].astype(jnp.float32), -LIMIT, LIMIT)]
    all_to_all x2 -> x0, waiting for transfers between devices: 135 us -> none  [the longest x1 69.3 us: local_block(): received = lax.all_to_all(rows, 'ep', 0, 0, tiled=True)]
    pallas_call x0 -> x3, Pallas kernels: none -> 119 us  [the longest x1 51.6 us: gate_up(): pl.pallas_call(functools.partial(gate_up_kernel, blk, m_blk, slots), out_...]
    dot_general x3 -> x0, matrix products: 91.8 us -> none  [the longest x1 56 us: local_block(): jnp.einsum('sgcd,gdf->gscf', received, w_gate_up, preferred_element_type=...]
    reduce_scatter x0 -> x1, waiting for transfers between devices: none -> 39.2 us  [local_block(): mixed = lax.psum_scatter(part, 'ep', scatter_dimension=0, tiled=True)]
    gather x6 -> x0, local copies, waits for them, and re-layouts: 15.8 us -> none  [the longest x2 7 us: local_block(): jnp.take(returned.reshape(-1, d_model), back_slot, axis=0)]
    all_to_all x2 -> x0, starting transfers between devices: 10.5 us -> none  [the longest x1 5.44 us: local_block(): received = lax.all_to_all(rows, 'ep', 0, 0, tiled=True)]
  transfers between devices with their start and end apart: 2 -> 1, of which waited for: 2 -> 1; matrix products, arithmetic and copies ran while one was open for 0% -> 0% of each run, Pallas kernels for 0% -> 0%
where the time goes in v1:
time: 182 us
  Pallas kernels  119 us (65%)
  waiting for transfers between devices  39.2 us (22%)
  between operations  13.5 us (7%)
  local copies, waits for them, and re-layouts  7.64 us (4%)
  other arithmetic  1.93 us (1%)
    pallas_call x1, Pallas kernels, gate_up(): pl.pallas_call(functools.partial(gate_up_kernel, blk, m_blk, slots), out_...  51.6 us
    pallas_call x1, Pallas kernels, down(): pl.pallas_call(functools.partial(down_kernel, blk, slots), out_shape=jax....  39.3 us
    reduce_scatter x1, waiting for transfers between devices, local_block(): mixed = lax.psum_scatter(part, 'ep', scatter_dimension=0, tiled=True)  39.2 us
    pallas_call x1, Pallas kernels, dispatch(): pl.pallas_call(functools.partial(dispatch_kernel, n, local_exp), out_shap...  28.5 us
  transfers between devices with their start and end apart: 1, of which 1 were waited for; matrix products, arithmetic and copies ran while one was open for 0% of the time, Pallas kernels for 0%

profile of v1, /device:TPU:112, one launch (start us, length us, event | category | flops | bytes accessed | tf_op | source)
XLA Modules:
  0.0 181.7 jit_solution(8560489796262224545)
XLA Ops:
  6.5 0.0 reduce-scatter.2.cloned.1.call-start
  6.6 1.3 reshape.15.g_ref
  7.9 1.4 copy.12.ids_ref
  9.2 1.4 copy.15.b_ref
  10.6 1.5 copy.14.b_ref
  12.1 2.1 %copy.13.wr_ref = bf16[2880,32]{1,0:T(8,128)(2,1)} copy(bf16[2880,32]{0,1:T(8,128)(2,1)} %param.12) | data formatting | bytes 368640 | tf_op args[3]
  14.2 28.5 %dispatch.1 = (bf16[8,64,2880]{2,1,0:T(8,128)(2,1)}, f32[512,8]{1,0:T(8,128)}, f32[8,512]{1,0:T(8,128)}, f32[512,4]{1,0:T(8,128)}) custom-call(bf16[64,2880]{1,0:T(8,128)(2,1)} %x_ref.1, s32[64,4]{1,0:T(8,128)} %copy.12.ids_ref, bf16[1,2880]{1,0:T(2,128)(2,1)} %reshape.15.g_ref, bf16[2880,32]{1,0:T(8,128)(2,1)} %copy.13.wr_ref, bf16[1,32]{1,0:T(2,128)(2,1)} %bitcast.7), custom_call_target="tpu_custom_call" | custom-call | tf_op jit(solution)/shard_map/dispatch/pallas_call | solution.py:142
  42.7 51.6 %gate_up.1.z_ref = bf16[4,256,2880]{2,1,0:T(8,128)(2,1)} custom-call(bf16[512,2880]{1,0:T(8,128)(2,1)} %bitcast.4, f32[8,512]{1,0:T(8,128)} %get-tuple-element.10.post_ref, bf16[4,2880,5760]{2,1,0:T(8,128)(2,1)} %w_hbm.2, bf16[4,1,5760]{2,1,0:T(2,128)(2,1)} %copy.14.b_ref), custom_call_target="tpu_custom_call" | custom-call | tf_op jit(solution)/shard_map/gate_up/pallas_call | solution.py:256
  94.3 39.3 %down.1 = f32[512,2880]{1,0:T(8,128)} custom-call(bf16[4,256,2880]{2,1,0:T(8,128)(2,1)} %gate_up.1.z_ref, f32[512,8]{1,0:T(8,128)} %get-tuple-element.11.pos_ref, f32[512,4]{1,0:T(8,128)} %get-tuple-element.12.p_ref, bf16[4,2880,2880]{2,1,0:T(8,128)(2,1)} %w_hbm.3, bf16[4,1,2880]{2,1,0:T(2,128)(2,1)} %copy.15.b_ref), custom_call_target="tpu_custom_call" | custom-call | tf_op jit(solution)/shard_map/down/pallas_call | solution.py:310
  133.7 0.0 copy-start
  133.7 0.1 reduce-scatter.2.cloned.1.call-update
  133.7 39.2 %reduce-scatter.2.cloned.1.call-done = f32[64,2880]{1,0:T(8,128)} async-done(((f32[512,2880]{1,0:T(8,128)}), f32[64,2880]{1,0:T(8,128)}) %reduce-scatter.2.cloned.1.call-update) | async-done | bytes 737296 | tf_op jit(solution)/shard_map/reduce_scatter | solution.py:337
  172.9 0.0 copy-done
  172.9 1.9 %add_convert_fusion = bf16[64,2880]{1,0:T(8,128)(2,1)} fusion(f32[64,2880]{1,0:T(8,128)} %reduce-scatter.2.cloned.1.call-done, bf16[64,2880]{1,0:T(8,128)(2,1)S(1)} %copy-done), kind=kLoop, calls=%fused_computation | loop fusion | flops 552960 | bytes 1474560 | tf_op jit(solution)/shard_map/convert_element_type | solution.py:338
Async XLA Ops:
  6.5 166.3 %reduce-scatter.2.cloned.1.call-start = ((), (), s32[]{:S(2)}) async-start(), calls=%async_computation.1 | async-start | bytes 6782976 | tf_op jit(solution)/shard_map/reduce_scatter | solution.py:337
  133.7 39.2 %copy-start = (bf16[64,2880]{1,0:T(8,128)(2,1)S(1)}, bf16[64,2880]{1,0:T(8,128)(2,1)}, u32[]{:S(2)}) copy-start(bf16[64,2880]{1,0:T(8,128)(2,1)} %x_ref.1) | copy-start | bytes 1105924
Sparse Core Ops, SparseCore 0:
  133.8 38.9 reduce-scatter.1

commit v2 on v1

--- a/solution.py
+++ b/solution.py
@@ -34,8 +34,12 @@
     right, left = right_chip * 2 + core, left_chip * 2 + core
     far = far_chip * 2 + core
     tok, _ = x_ref.shape
-    top_k = ids_ref.shape[1]
-    experts = wr_ref.shape[1]
+    top_k = ids_ref.shape[0]
+    experts = wr_ref.shape[0]
+
+    def at(dev):
+        return (dev % 2) * chips + dev // 2
+
     half = tok // 2
 
     barrier = pltpu.get_barrier_semaphore()
@@ -44,11 +48,14 @@
 
     x = x_ref[...].astype(F32)
     inv = lax.rsqrt(jnp.mean(x * x, axis=-1, keepdims=True) + EPSILON)
-    h = (x * inv * g_ref[...].astype(F32)).astype(BF16)
-    hall[me] = h
-    logits = dot32(h, wr_ref[...]) + br_ref[...].astype(F32)
-    lane = lax.broadcasted_iota(jnp.int32, (tok, experts), 1)
-    hot = [ids_ref[:, k:k + 1] == lane for k in range(top_k)]
+    h = (x * inv * g_ref[...].astype(F32)[None, :]).astype(BF16)
+    hall[at(me)] = h
+    logits = lax.dot_general(h, wr_ref[...], (((1,), (1,)), ((), ())), preferred_element_type=F32) + br_ref[...].astype(F32)[None, :]
+    ids = ids_ref[...]
+    expert = lax.broadcasted_iota(jnp.int32, (experts, tok), 0)
+    turn = jnp.where(lax.broadcasted_iota(jnp.int32, (experts, experts), 0)
+                     == lax.broadcasted_iota(jnp.int32, (experts, experts), 1), 1.0, 0.0).astype(BF16)
+    hot = [dot_t(jnp.where(ids[k:k + 1, :] == expert, 1.0, 0.0).astype(BF16), turn) > 0.5 for k in range(top_k)]
     picked = [jnp.sum(jnp.where(hk, logits, 0.0), axis=1, keepdims=True) for hk in hot]
     top = functools.reduce(jnp.maximum, picked)
     ex = [jnp.exp(v - top) for v in picked]
@@ -58,8 +65,8 @@
     for k in range(top_k):
         gates = gates + jnp.where(hot[k], ex[k] / total, 0.0)
         chosen = chosen + jnp.where(hot[k], 1.0, 0.0)
-    mall[me, 0] = gates
-    mall[me, 1] = chosen
+    mall[at(me), 0] = gates
+    mall[at(me), 1] = chosen
 
     pl.semaphore_wait(barrier, n - 1)
 
@@ -76,31 +83,31 @@
 
     for i, (dev, parts) in enumerate(((right, (lo, hi)), (left, (hi, lo)))):
         for j, rows in enumerate(parts):
-            start(copy(hall.at[me, rows], hall.at[me, rows], sb.at[i, j], rb.at[i, j], dev))
-    start(copy(hall.at[me], hall.at[me], sa, ra, partner))
+            start(copy(hall.at[at(me), rows], hall.at[at(me), rows], sb.at[i, j], rb.at[i, j], dev))
+    start(copy(hall.at[at(me)], hall.at[at(me)], sa, ra, partner))
     metas = []
     for k in range(1, n):
-        c = copy(mall.at[me], mall.at[me], sm.at[k - 1], rm.at[k - 1], (me + k) % n)
+        c = copy(mall.at[at(me)], mall.at[at(me)], sm.at[k - 1], rm.at[k - 1], (me + k) % n)
         c.start()
         metas.append(c)
     order = ((0, left, right, (lo, hi)), (1, right, left, (hi, lo)))
     for i, origin, onward, parts in order:
-        slot = hall.at[origin, parts[0]]
+        slot = hall.at[at(origin), parts[0]]
         copy(slot, slot, sb.at[i, 0], rb.at[i, 0], origin).wait_recv()
         start(copy(slot, slot, sc.at[i], rc.at[i], onward))
         start(copy(slot, slot, sd.at[i, 0], rd.at[i, 0], partner))
     for i, origin, onward, parts in order:
-        slot = hall.at[origin, parts[1]]
+        slot = hall.at[at(origin), parts[1]]
         copy(slot, slot, sb.at[i, 1], rb.at[i, 1], origin).wait_recv()
         start(copy(slot, slot, sd.at[i, 1], rd.at[i, 1], partner))
     for i, origin, onward, parts in order:
-        slot = hall.at[far, parts[0]]
+        slot = hall.at[at(far), parts[0]]
         copy(slot, slot, sc.at[i], rc.at[i], origin).wait_recv()
         start(copy(slot, slot, sd.at[i, 2], rd.at[i, 2], partner))
 
     for k in range(1, n):
         src = (me + n - k) % n
-        copy(mall.at[src], mall.at[src], sm.at[k - 1], rm.at[k - 1], src).wait_recv()
+        copy(mall.at[at(src)], mall.at[at(src)], sm.at[k - 1], rm.at[k - 1], src).wait_recv()
     tokens = n * tok
     e0 = me * local_exp
     gates_all = mall[:, 0].reshape(tokens, experts)
@@ -120,13 +127,13 @@
     for e in range(local_exp):
         p_ref[:, e:e + 1] = jnp.sum(jnp.where(lane_all == e0 + e, gates_all, 0.0), axis=1, keepdims=True)
 
-    copy(hall.at[partner], hall.at[partner], sa, ra, partner).wait_recv()
+    copy(hall.at[at(partner)], hall.at[at(partner)], sa, ra, partner).wait_recv()
     for i, origin_chip, parts in ((0, left_chip, (lo, hi)), (1, right_chip, (hi, lo))):
         other = origin_chip * 2 + (1 - core)
         for j in range(2):
-            slot = hall.at[other, parts[j]]
+            slot = hall.at[at(other), parts[j]]
             copy(slot, slot, sd.at[i, j], rd.at[i, j], partner).wait_recv()
-        slot = hall.at[far_chip * 2 + (1 - core), parts[0]]
+        slot = hall.at[at(far_chip * 2 + (1 - core)), parts[0]]
         copy(slot, slot, sd.at[i, 2], rd.at[i, 2], partner).wait_recv()
     for c in sends:
         c.wait_send()
@@ -147,7 +154,7 @@
                    jax.ShapeDtypeStruct((tokens, local_exp), F32)),
         in_specs=[vm] * 5,
         out_specs=(vm,) * 4,
-        scratch_shapes=[pltpu.VMEM((n, 2, tok, wr.shape[1]), F32),
+        scratch_shapes=[pltpu.VMEM((n, 2, tok, wr.shape[0]), F32),
                         dma, dma, dma((2, 2)), dma((2, 2)), dma((2,)), dma((2,)), dma((2, 3)), dma((2, 3)),
                         dma((n - 1,)), dma((n - 1,))],
         compiler_params=pltpu.CompilerParams(collective_id=0, has_side_effects=True, vmem_limit_bytes=VMEM_LIMIT),
@@ -156,7 +163,7 @@
     return hall.reshape(tokens, d_model), pos, post, p
 
 
-def gate_up_kernel(blk, m_blk, slots, hall, post_ref, w_hbm, b_ref, z_ref, wbuf, xg, perm, sems):
+def gate_up_kernel(blk, m_blk, slots, hall, post_ref, w_hbm, b_ref, z_ref, wbuf, xg, perm, bias_ref, sems):
     local_exp, d_model, width = w_hbm.shape
     full, rest = width // blk, width % blk
     per_exp = full + (1 if rest else 0)
@@ -164,6 +171,7 @@
     tokens = hall.shape[0]
     depth = slots - 1
 
+    bias_ref[...] = b_ref[...].astype(F32)
     src = lax.broadcasted_iota(jnp.int32, (256, 256), 0)
     dst = lax.broadcasted_iota(jnp.int32, (256, 256), 1)
     want = jnp.where(dst < 128, 2 * dst, 2 * (dst - 128) + 1)
@@ -217,7 +225,7 @@
 
             block_copy(q, cols != blk).wait()
             off = pl.multiple_of(j * blk, 128)
-            bias = b_ref[e, :, pl.ds(off, cols)].astype(F32)
+            bias = bias_ref[pl.ds(e, 1), pl.ds(off, cols)]
 
             def rows(m, c):
                 at = pl.ds(pl.multiple_of(m * m_blk, m_blk), m_blk)
@@ -259,65 +267,171 @@
         in_specs=[vm, vm, pl.BlockSpec(memory_space=pl.ANY), vm],
         out_specs=vm,
         scratch_shapes=[pltpu.VMEM((slots, d_model, blk), BF16), pltpu.VMEM((max_rows, d_model), BF16),
-                        pltpu.VMEM((256, 256), BF16), pltpu.SemaphoreType.DMA((slots,))],
+                        pltpu.VMEM((256, 256), BF16), pltpu.VMEM((local_exp, width), F32), pltpu.SemaphoreType.DMA((slots,))],
         compiler_params=pltpu.CompilerParams(vmem_limit_bytes=VMEM_LIMIT),
         name='gate_up',
-    )(hall, post, w, b.reshape(local_exp, 1, width))
-
-
-def down_kernel(blk, slots, z_ref, pos_ref, p_ref, w_hbm, b_ref, out_ref, wbuf, wrest, scat, sems, rsems):
+    )(hall, post, w, b)
+
+
+def down_kernel(n, chunks, slots, z_ref, pos_ref, p_ref, x_ref, b_ref, w_hbm, out_ref,
+                wbuf, wrest, scat, part, part_r, near, near_r, ring, ring_r,
+                wsem, rsem, ns, nr, fs, fr, hs, hr):
     local_exp, d_ff, width = w_hbm.shape
     tokens = pos_ref.shape[0]
     max_rows = z_ref.shape[1]
-    chunks = [(c, min(blk, width - c)) for c in range(0, width, blk)]
+    tok = tokens // n
+    half = tok // 2
+    nchip = n // 2
+    blk = chunks[0][1]
     total = len(chunks) * local_exp
     depth = slots - 1
+    me = lax.axis_index('ep')
+    chip, core = me // 2, me % 2
+    partner = chip * 2 + (1 - core)
+    right_chip, left_chip, far_chip = (chip + 1) % nchip, (chip + nchip - 1) % nchip, (chip + 2) % nchip
+    right, left = right_chip * 2 + core, left_chip * 2 + core
+    sides = ((right, right_chip, 0), (left, left_chip, 1))
+
+    barrier = pltpu.get_barrier_semaphore()
+    for dev in (partner, right, left):
+        pl.semaphore_signal(barrier, inc=1, device_id={'ep': dev}, device_id_type=pl.DeviceIdType.MESH)
 
     def block_copy(q):
         off, cols = chunks[q // local_exp]
         src = w_hbm.at[q % local_exp, :, pl.ds(off, cols)]
         if cols == blk:
-            return pltpu.make_async_copy(src, wbuf.at[q % slots], sems.at[q % slots])
-        return pltpu.make_async_copy(src, wrest.at[q % local_exp], rsems.at[q % local_exp])
+            return pltpu.make_async_copy(src, wbuf.at[q % slots], wsem.at[q % slots])
+        return pltpu.make_async_copy(src, wrest.at[q % local_exp], rsem.at[q % local_exp])
 
     for q in range(depth):
         block_copy(q).start()
+
+    def copy(src, dst, ssem, rsem_, dev):
+        return pltpu.make_async_remote_copy(src_ref=src, dst_ref=dst, send_sem=ssem, recv_sem=rsem_,
+                                            device_id={'ep': dev}, device_id_type=pl.DeviceIdType.MESH)
+
+    def bufs(c):
+        if chunks[c][1] == blk:
+            return part.at[c], near.at[c], ring.at[c]
+        return part_r, near_r, ring_r
+
+    def near_copy(c):
+        pb, nb, _ = bufs(c)
+        return copy(pb.at[1 - core], nb, ns.at[c], nr.at[c], partner)
+
+    def far_copy(c, side):
+        dev, _, i = side
+        pb, _, rb = bufs(c)
+        rows = pl.ds(i * half, half)
+        return copy(pb.at[core, far_chip, rows], rb.at[i, 0], fs.at[c, i, 0], fr.at[c, i, 0], dev)
+
+    def early_copy(c, side):
+        dev, dchip, i = side
+        pb, _, rb = bufs(c)
+        rows = pl.ds((1 - i) * half, half)
+        return copy(pb.at[core, dchip, rows], rb.at[i, 1], fs.at[c, i, 1], fr.at[c, i, 1], dev)
+
+    def late_copy(c, side):
+        dev, dchip, i = side
+        pb, _, rb = bufs(c)
+        rows = pl.ds(i * half, half)
+        return copy(pb.at[core, dchip, rows], rb.at[i, 2], hs.at[c, i], hr.at[c, i], dev)
+
+    def stage_near(c):
+        near_copy(c).start()
+
+    def stage_far(c):
+        near_copy(c).wait()
+        pb, nb, _ = bufs(c)
+        pb[core] += nb[...]
+        for side in sides:
+            far_copy(c, side).start()
+            early_copy(c, side).start()
+
+    def stage_late(c):
+        pb, _, rb = bufs(c)
+        for side in sides:
+            _, dchip, i = side
+            far_copy(c, side).wait_recv()
+            pb[core, dchip, i * half:(i + 1) * half] += rb[i, 0]
+            late_copy(c, side).start()
+
+    def stage_out(c):
+        off, cols = chunks[c]
+        pb, _, rb = bufs(c)
+        for side in sides:
+            early_copy(c, side).wait_recv()
+            late_copy(c, side).wait_recv()
+        for r in range(2):
+            rows = slice(r * half, (r + 1) * half)
+            total_ = pb[core, chip, rows] + rb[0, 2 if r == 0 else 1] + rb[1, 1 if r == 0 else 2]
+            out_ref[rows, off:off + cols] = (x_ref[rows, off:off + cols].astype(F32) + total_).astype(BF16)
+
     slot_ids = lax.broadcasted_iota(jnp.int32, (tokens, max_rows), 1).astype(F32)
     for e in range(local_exp):
         scat[e] = jnp.where(pos_ref[:, e:e + 1] == slot_ids, 1.0, 0.0).astype(BF16)
     row_ids = lax.broadcasted_iota(jnp.int32, (max_rows, 1), 0).astype(F32)
+    counts = [jnp.max(pos_ref[:, e:e + 1]) + 1.0 for e in range(local_exp)]
+    bias = b_ref[...].astype(F32)
+    pl.semaphore_wait(barrier, 3)
+
+    last = len(chunks)
     for c, (off, cols) in enumerate(chunks):
+        pb = bufs(c)[0]
         for e in range(local_exp):
             q = c * local_exp + e
             if q + depth < total:
                 block_copy(q + depth).start()
             block_copy(q).wait()
-            count = jnp.max(pos_ref[:, e:e + 1]) + 1.0
             wv = wbuf[q % slots] if cols == blk else wrest[e]
-            y = dot32(z_ref[e], wv) + b_ref[e, :, off:off + cols].astype(F32)
-            y = jnp.where(row_ids < count, y, 0.0).astype(BF16)
-            part = p_ref[:, e:e + 1] * dot32(scat[e], y)
+            y = dot32(z_ref[e], wv) + bias[e:e + 1, off:off + cols]
+            y = jnp.where(row_ids < counts[e], y, 0.0).astype(BF16)
+            add = (p_ref[:, e:e + 1] * dot32(scat[e], y)).reshape(2, nchip, tok, cols)
             if e == 0:
-                out_ref[:, off:off + cols] = part
+                pb[...] = add
             else:
-                out_ref[:, off:off + cols] += part
-
-
-def down(z, pos, p, w, b, blk, slots):
+                pb[...] += add
+            if e == 0 and c >= 2:
+                stage_out(c - 2)
+            if e == 1 and c >= 1:
+                stage_far(c - 1)
+            if e == 3 and c >= 1:
+                stage_late(c - 1)
+        stage_near(c)
+    stage_far(last - 1)
+    stage_out(last - 2)
+    stage_late(last - 1)
+    stage_out(last - 1)
+    for c in range(last):
+        for side in sides:
+            far_copy(c, side).wait_send()
+            early_copy(c, side).wait_send()
+            late_copy(c, side).wait_send()
+
+
+def down(z, pos, p, x, w, b, n, blk, slots):
     local_exp, d_ff, width = w.shape
     tokens = pos.shape[0]
+    tok = tokens // n
+    chunks = [(c, min(blk, width - c)) for c in range(0, width, blk)]
+    full, rest, last = width // blk, width % blk, len(chunks)
     vm = pl.BlockSpec(memory_space=pltpu.VMEM)
+    dma = pltpu.SemaphoreType.DMA
     return pl.pallas_call(
-        functools.partial(down_kernel, blk, slots),
-        out_shape=jax.ShapeDtypeStruct((tokens, width), F32),
-        in_specs=[vm, vm, vm, pl.BlockSpec(memory_space=pl.ANY), vm],
+        functools.partial(down_kernel, n, chunks, slots),
+        out_shape=jax.ShapeDtypeStruct((tok, width), BF16),
+        in_specs=[vm, vm, vm, vm, vm, pl.BlockSpec(memory_space=pl.ANY)],
         out_specs=vm,
-        scratch_shapes=[pltpu.VMEM((slots, d_ff, blk), BF16), pltpu.VMEM((local_exp, d_ff, width % blk), BF16),
+        scratch_shapes=[pltpu.VMEM((slots, d_ff, blk), BF16), pltpu.VMEM((local_exp, d_ff, rest), BF16),
                         pltpu.VMEM((local_exp, tokens, z.shape[1]), BF16),
-                        pltpu.SemaphoreType.DMA((slots,)), pltpu.SemaphoreType.DMA((local_exp,))],
-        compiler_params=pltpu.CompilerParams(vmem_limit_bytes=VMEM_LIMIT),
+                        pltpu.VMEM((full, 2, n // 2, tok, blk), F32), pltpu.VMEM((2, n // 2, tok, rest), F32),
+                        pltpu.VMEM((full, n // 2, tok, blk), F32), pltpu.VMEM((n // 2, tok, rest), F32),
+                        pltpu.VMEM((full, 2, 3, tok // 2, blk), F32), pltpu.VMEM((2, 3, tok // 2, rest), F32),
+                        dma((slots,)), dma((local_exp,)),
+                        dma((last,)), dma((last,)), dma((last, 2, 2)), dma((last, 2, 2)), dma((last, 2)), dma((last, 2))],
+        compiler_params=pltpu.CompilerParams(collective_id=1, has_side_effects=True, vmem_limit_bytes=VMEM_LIMIT),
         name='down',
-    )(z, pos, p, w, b.reshape(local_exp, 1, width))
+    )(z, pos, p, x, b, w)
 
 
 def solution(mesh):
@@ -331,10 +445,8 @@
         experts = local_exp * n
         max_rows = n * (4 * top_k * tok // experts)
         blk = 768 if w_gate_up.shape[2] >= 2048 else 256
-        hall, pos, post, p = dispatch(x_in, expert_ids, norm_weight.reshape(1, -1), router_w, router_b.reshape(1, -1), n, local_exp)
+        hall, pos, post, p = dispatch(x_in, expert_ids.T, norm_weight, router_w.T, router_b, n, local_exp)
         z = gate_up(hall, post, w_gate_up, b_gate_up, max_rows, blk, min(128, max_rows), 4)
-        part = down(z, pos, p, w_down, b_down, blk, 4)
-        mixed = lax.psum_scatter(part, 'ep', scatter_dimension=0, tiled=True)
-        return (x_in.astype(F32) + mixed).astype(BF16)
+        return down(z, pos, p, x_in, w_down, b_down, n, 512 if blk == 768 else 128, 4)
 
     return jax.shard_map(local_block, mesh=mesh, in_specs=(rows_spec, rows_spec, P(), P(), P(), P('ep', None, None), P('ep', None), P('ep', None, None), P('ep', None)), out_specs=rows_spec, check_vma=False)

time: 182 us -> 150 us (0.82)
  waiting for transfers between devices: 39.2 us -> 0 us
  Pallas kernels: 119 us -> 149 us
  between operations: 13.5 us -> 0.03 us
  local copies, waits for them, and re-layouts: 7.64 us -> 1.76 us
  other arithmetic: 1.93 us -> 0 us
    reduce_scatter x1 -> x0, waiting for transfers between devices: 39.2 us -> none  [local_block(): mixed = lax.psum_scatter(part, 'ep', scatter_dimension=0, tiled=True)]
    pallas_call x1, Pallas kernels: 39.3 us -> 69.4 us  [down(): pl.pallas_call(functools.partial(down_kernel, n, chunks, slots), out_shap...]
    reshape x3 -> x0, local copies, waits for them, and re-layouts: 4.19 us -> none  [the longest x1 1.5 us: gate_up(): b.reshape(local_exp, 1, width)]
    convert_element_type x1 -> x0, other arithmetic: 1.93 us -> none  [local_block(): return (x_in.astype(F32) + mixed).astype(BF16)]
  transfers between devices with their start and end apart: 1 -> 0, of which waited for: 1 -> 0; matrix products, arithmetic and copies ran while one was open for 0% -> 0% of each run, Pallas kernels for 0% -> 0%
where the time goes in v2:
time: 150 us; the launch traced here: 151 us
  Pallas kernels  149 us (99%)
  local copies, waits for them, and re-layouts  1.76 us (1%)
    pallas_call x1, Pallas kernels, down(): pl.pallas_call(functools.partial(down_kernel, n, chunks, slots), out_shap...  69.4 us
    pallas_call x1, Pallas kernels, gate_up(): pl.pallas_call(functools.partial(gate_up_kernel, blk, m_blk, slots), out_...  51.6 us
    pallas_call x1, Pallas kernels, dispatch(): pl.pallas_call(functools.partial(dispatch_kernel, n, local_exp), out_shap...  28.3 us

profile of v2, /device:TPU:112, one launch (start us, length us, event | category | flops | bytes accessed | tf_op | source)
XLA Modules:
  0.0 151.1 jit_solution(10990632892873992457)
XLA Ops:
  0.0 28.3 %dispatch.1 = (bf16[8,64,2880]{2,1,0:T(8,128)(2,1)}, f32[512,8]{1,0:T(8,128)}, f32[8,512]{1,0:T(8,128)}, f32[512,4]{1,0:T(8,128)}) custom-call(bf16[64,2880]{1,0:T(8,128)(2,1)} %x_ref.3, s32[4,64]{1,0:T(4,128)} %bitcast.5, bf16[2880]{0:T(1024)(128)(2,1)} %g_ref.1, bf16[32,2880]{1,0:T(8,128)(2,1)} %bitcast.4, bf16[32]{0:T(256)(128)(2,1)} %br_ref.1), custom_call_target="tpu_custom_call" | custom-call | tf_op jit(solution)/shard_map/dispatch/pallas_call | solution.py:149
  28.3 51.6 %gate_up.1.z_ref = bf16[4,256,2880]{2,1,0:T(8,128)(2,1)} custom-call(bf16[512,2880]{1,0:T(8,128)(2,1)} %bitcast.3, f32[8,512]{1,0:T(8,128)} %get-tuple-element.10.post_ref, bf16[4,2880,5760]{2,1,0:T(8,128)(2,1)} %w_hbm.2, bf16[4,5760]{1,0:T(4,128)(2,1)} %b_ref.2), custom_call_target="tpu_custom_call" | custom-call | tf_op jit(solution)/shard_map/gate_up/pallas_call | solution.py:264
  79.9 69.4 %down.1 = bf16[64,2880]{1,0:T(8,128)(2,1)} custom-call(bf16[4,256,2880]{2,1,0:T(8,128)(2,1)} %gate_up.1.z_ref, f32[512,8]{1,0:T(8,128)} %get-tuple-element.11.pos_ref, f32[512,4]{1,0:T(8,128)} %get-tuple-element.12.p_ref, bf16[64,2880]{1,0:T(8,128)(2,1)} %x_ref.3, bf16[4,2880]{1,0:T(4,128)(2,1)} %b_ref.3, bf16[4,2880,2880]{2,1,0:T(8,128)(2,1)} %w_hbm.3), custom_call_target="tpu_custom_call" | custom-call | tf_op jit(solution)/shard_map/down/pallas_call | solution.py:420
  149.4 1.8 %copy.11 = bf16[64,2880]{1,0:T(8,128)(2,1)} copy(bf16[64,2880]{1,0:T(8,128)(2,1)} %down.1) | data formatting | bytes 737280

commit v3 on v2

--- a/solution.py
+++ b/solution.py
@@ -12,19 +12,25 @@
 ALPHA = 1.702
 F32 = jnp.float32
 BF16 = jnp.bfloat16
-VMEM_LIMIT = 63 * 1024 * 1024
+DISPATCH_VMEM = 10 * 1024 * 1024
+GATE_UP_VMEM = 20 * 1024 * 1024
+DOWN_VMEM = 48 * 1024 * 1024
 
 
 def dot32(a, b):
     return jnp.dot(a, b, preferred_element_type=F32)
 
 
+def in_vmem(a):
+    return pltpu.with_memory_space_constraint(a, pltpu.VMEM)
+
+
 def dot_t(a, b):
     return lax.dot_general(a, b, (((0,), (0,)), ((), ())), preferred_element_type=F32)
 
 
-def dispatch_kernel(n, local_exp, x_ref, ids_ref, g_ref, wr_ref, br_ref, hall, pos_ref, post_ref, p_ref,
-                    mall, sa, ra, sb, rb, sc, rc, sd, rd, sm, rm):
+def dispatch_kernel(n, local_exp, x_ref, ids_ref, g_ref, wr_ref, br_ref, w_hbm, hall, pos_ref, post_ref, p_ref, pre,
+                    mall, psem, sa, ra, sb, rb, sc, rc, sd, rd, sm, rm):
     me = lax.axis_index('ep')
     chips = n // 2
     chip, core = me // 2, me % 2
@@ -45,6 +51,10 @@
     barrier = pltpu.get_barrier_semaphore()
     for k in range(1, n):
         pl.semaphore_signal(barrier, inc=1, device_id={'ep': (me + k) % n}, device_id_type=pl.DeviceIdType.MESH)
+    blk = pre.shape[2]
+    ahead = [pltpu.make_async_copy(w_hbm.at[0, :, pl.ds(j * blk, blk)], pre.at[j], psem.at[j]) for j in range(pre.shape[0])]
+    for c in ahead:
+        c.start()
 
     x = x_ref[...].astype(F32)
     inv = lax.rsqrt(jnp.mean(x * x, axis=-1, keepdims=True) + EPSILON)
@@ -139,43 +149,38 @@
         c.wait_send()
     for c in metas:
         c.wait_send()
-
-
-def dispatch(x, ids, g, wr, br, n, local_exp):
+    for c in ahead:
+        c.wait()
+
+
+def dispatch(x, ids, g, wr, br, w, n, local_exp, blk, npre):
     tok, d_model = x.shape
     tokens = n * tok
     vm = pl.BlockSpec(memory_space=pltpu.VMEM)
     dma = pltpu.SemaphoreType.DMA
-    hall, pos, post, p = pl.pallas_call(
+    hall, pos, post, p, pre = pl.pallas_call(
         functools.partial(dispatch_kernel, n, local_exp),
-        out_shape=(jax.ShapeDtypeStruct((n, tok, d_model), BF16),
-                   jax.ShapeDtypeStruct((tokens, 8), F32),
-                   jax.ShapeDtypeStruct((8, tokens), F32),
-                   jax.ShapeDtypeStruct((tokens, local_exp), F32)),
-        in_specs=[vm] * 5,
-        out_specs=(vm,) * 4,
-        scratch_shapes=[pltpu.VMEM((n, 2, tok, wr.shape[0]), F32),
+        out_shape=(pltpu.VMEM((n, tok, d_model), BF16), pltpu.VMEM((tokens, 8), F32), pltpu.VMEM((8, tokens), F32),
+                   pltpu.VMEM((tokens, local_exp), F32), pltpu.VMEM((npre, d_model, blk), BF16)),
+        in_specs=[vm] * 5 + [pl.BlockSpec(memory_space=pl.ANY)],
+        out_specs=(vm,) * 5,
+        scratch_shapes=[pltpu.VMEM((n, 2, tok, wr.shape[0]), F32), dma((npre,)),
                         dma, dma, dma((2, 2)), dma((2, 2)), dma((2,)), dma((2,)), dma((2, 3)), dma((2, 3)),
                         dma((n - 1,)), dma((n - 1,))],
-        compiler_params=pltpu.CompilerParams(collective_id=0, has_side_effects=True, vmem_limit_bytes=VMEM_LIMIT),
+        compiler_params=pltpu.CompilerParams(collective_id=0, has_side_effects=True, vmem_limit_bytes=DISPATCH_VMEM),
         name='dispatch',
-    )(x, ids, g, wr, br)
-    return hall.reshape(tokens, d_model), pos, post, p
-
-
-def gate_up_kernel(blk, m_blk, slots, hall, post_ref, w_hbm, b_ref, z_ref, wbuf, xg, perm, bias_ref, sems):
+    )(x, ids, g, wr, br, w)
+    return hall, pos, post, p, pre
+
+
+def gate_up_kernel(m_blk, slots, hall, post_ref, pre, b_ref, w_hbm, z_ref, wbuf, xg, perm, bias_ref, sems):
     local_exp, d_model, width = w_hbm.shape
+    npre, _, blk = pre.shape
     full, rest = width // blk, width % blk
     per_exp = full + (1 if rest else 0)
     total = local_exp * per_exp
-    tokens = hall.shape[0]
+    tokens = hall.shape[0] * hall.shape[1]
     depth = slots - 1
-
-    bias_ref[...] = b_ref[...].astype(F32)
-    src = lax.broadcasted_iota(jnp.int32, (256, 256), 0)
-    dst = lax.broadcasted_iota(jnp.int32, (256, 256), 1)
-    want = jnp.where(dst < 128, 2 * dst, 2 * (dst - 128) + 1)
-    perm[...] = jnp.where(src == want, 1.0, 0.0).astype(BF16)
 
     def block_copy(q, is_rest):
         e, j = q // per_exp, q % per_exp
@@ -186,91 +191,114 @@
         return pltpu.make_async_copy(w_hbm.at[e, :, pl.ds(pl.multiple_of(j * blk, 128), blk)], wbuf.at[slot], sems.at[slot])
 
     def start(q):
-        if not rest:
-            block_copy(q, False).start()
-            return
-        j = lax.rem(q, per_exp)
+        j = q % per_exp
 
         @pl.when(j < full)
         def _():
             block_copy(q, False).start()
 
-        @pl.when(j == full)
-        def _():
-            block_copy(q, True).start()
-
-    for q in range(depth):
-        start(jnp.int32(q))
-
-    def one_expert(e, carry):
+        if rest:
+            @pl.when(j == full)
+            def _():
+                block_copy(q, True).start()
+
+    for q in range(npre, npre + depth):
+        start(q)
+
+    bias_ref[...] = b_ref[...].astype(F32)
+    src = lax.broadcasted_iota(jnp.int32, (256, 256), 0)
+    dst = lax.broadcasted_iota(jnp.int32, (256, 256), 1)
+    want = jnp.where(dst < 128, 2 * dst, 2 * (dst - 128) + 1)
+    perm[...] = jnp.where(src == want, 1.0, 0.0).astype(BF16)
+
+    def gather(e):
         where_row = post_ref[pl.ds(e, 1), :]
         count = jnp.sum(jnp.where(where_row >= 0.0, 1.0, 0.0)).astype(jnp.int32)
         chunks = (count + (m_blk - 1)) // m_blk
 
-        def gather(m, c):
+        def body(m, c):
             at = lax.broadcasted_iota(jnp.int32, (m_blk, tokens), 0) + m * m_blk
             onehot = jnp.where(at.astype(F32) == where_row, 1.0, 0.0).astype(BF16)
-            xg[pl.ds(pl.multiple_of(m * m_blk, m_blk), m_blk), :] = dot32(onehot, hall[...]).astype(BF16)
+            xg[pl.ds(pl.multiple_of(m * m_blk, m_blk), m_blk), :] = dot32(onehot, hall[...].reshape(tokens, d_model)).astype(BF16)
             return c
 
-        lax.fori_loop(0, chunks, gather, 0)
-
-        def block(j, cols):
-            q = e * per_exp + j
-            slot = lax.rem(q, slots)
-
-            @pl.when(q + depth < total)
-            def _():
-                start(q + depth)
-
-            block_copy(q, cols != blk).wait()
-            off = pl.multiple_of(j * blk, 128)
-            bias = bias_ref[pl.ds(e, 1), pl.ds(off, cols)]
-
-            def rows(m, c):
-                at = pl.ds(pl.multiple_of(m * m_blk, m_blk), m_blk)
-                u = (dot32(xg[at, :], wbuf[slot, :, :cols]) + bias).astype(BF16)
-                for t in range(0, cols, 256):
-                    wide = min(256, cols - t)
-                    if wide == 256:
-                        pm = perm[...]
-                    else:
-                        pm = jnp.concatenate([perm[:128, :64], perm[:128, 128:192]], axis=1)
-                    al = dot32(u[:, t:t + wide], pm)
-                    gate = jnp.minimum(al[:, :wide // 2], LIMIT)
-                    linear = jnp.clip(al[:, wide // 2:], -LIMIT, LIMIT)
-                    z = gate * jax.nn.sigmoid(ALPHA * gate) * (linear + 1.0)
-                    zoff = pl.multiple_of(j * (blk // 2), 128) + t // 2
-                    z_ref[e, at, pl.ds(zoff, wide // 2)] = z.astype(BF16)
-                return c
-
-            lax.fori_loop(0, chunks, rows, 0)
+        lax.fori_loop(0, chunks, body, 0)
+        return chunks
+
+    def compute(e, j, cols, chunks, weights):
+        off = pl.multiple_of(j * blk, 128)
+        bias = bias_ref[pl.ds(e, 1), pl.ds(off, cols)]
+
+        def rows(m, c):
+            at = pl.ds(pl.multiple_of(m * m_blk, m_blk), m_blk)
+            u = (dot32(xg[at, :], weights()) + bias).astype(BF16)
+            for t in range(0, cols, 256):
+                wide = min(256, cols - t)
+                if wide == 256:
+                    pm = perm[...]
+                else:
+                    pm = jnp.concatenate([perm[:128, :64], perm[:128, 128:192]], axis=1)
+                al = dot32(u[:, t:t + wide], pm)
+                gate = jnp.minimum(al[:, :wide // 2], LIMIT)
+                linear = jnp.clip(al[:, wide // 2:], -LIMIT, LIMIT)
+                z = gate * jax.nn.sigmoid(ALPHA * gate) * (linear + 1.0)
+                zoff = pl.multiple_of(j * (blk // 2), 128) + t // 2
+                z_ref[e, at, pl.ds(zoff, wide // 2)] = z.astype(BF16)
+            return c
+
+        lax.fori_loop(0, chunks, rows, 0)
+
+    def streamed(e, j, cols, chunks):
+        q = e * per_exp + j
+        slot = q % slots
+
+        @pl.when(q + depth < total)
+        def _():
+            start(q + depth)
+
+        block_copy(q, cols != blk).wait()
+        compute(e, j, cols, chunks, lambda: wbuf[slot, :, :cols])
+
+    def expert(e, first):
+        chunks = gather(e)
+
+        def from_pre(j, c):
+            compute(e, j, blk, chunks, lambda: pre[j])
+            return c
 
         def body(j, c):
-            block(j, blk)
+            streamed(e, j, blk, chunks)
             return c
 
-        lax.fori_loop(0, full, body, 0)
+        if first:
+            lax.fori_loop(0, npre, from_pre, 0)
+        lax.fori_loop(npre if first else 0, full, body, 0)
         if rest:
-            block(jnp.int32(full), rest)
-        return carry
-
-    lax.fori_loop(0, local_exp, one_expert, 0)
-
-
-def gate_up(hall, post, w, b, max_rows, blk, m_blk, slots):
+            streamed(e, jnp.int32(full), rest, chunks)
+
+    expert(0, True)
+
+    def others(e, c):
+        expert(e, False)
+        return c
+
+    lax.fori_loop(1, local_exp, others, 0)
+
+
+def gate_up(hall, post, pre, w, b, max_rows, m_blk, slots):
     local_exp, d_model, width = w.shape
+    blk = pre.shape[2]
     vm = pl.BlockSpec(memory_space=pltpu.VMEM)
     return pl.pallas_call(
-        functools.partial(gate_up_kernel, blk, m_blk, slots),
-        out_shape=jax.ShapeDtypeStruct((local_exp, max_rows, width // 2), BF16),
-        in_specs=[vm, vm, pl.BlockSpec(memory_space=pl.ANY), vm],
+        functools.partial(gate_up_kernel, m_blk, slots),
+        out_shape=pltpu.VMEM((local_exp, max_rows, width // 2), BF16),
+        in_specs=[vm, vm, vm, vm, pl.BlockSpec(memory_space=pl.ANY)],
         out_specs=vm,
         scratch_shapes=[pltpu.VMEM((slots, d_model, blk), BF16), pltpu.VMEM((max_rows, d_model), BF16),
                         pltpu.VMEM((256, 256), BF16), pltpu.VMEM((local_exp, width), F32), pltpu.SemaphoreType.DMA((slots,))],
-        compiler_params=pltpu.CompilerParams(vmem_limit_bytes=VMEM_LIMIT),
+        compiler_params=pltpu.CompilerParams(vmem_limit_bytes=GATE_UP_VMEM),
         name='gate_up',
-    )(hall, post, w, b)
+    )(in_vmem(hall), in_vmem(post), in_vmem(pre), b, w)
 
 
 def down_kernel(n, chunks, slots, z_ref, pos_ref, p_ref, x_ref, b_ref, w_hbm, out_ref,
@@ -391,14 +419,17 @@
                 pb[...] = add
             else:
                 pb[...] += add
-            if e == 0 and c >= 2:
-                stage_out(c - 2)
-            if e == 1 and c >= 1:
-                stage_far(c - 1)
-            if e == 3 and c >= 1:
-                stage_late(c - 1)
+            if e == 1:
+                if c >= 1:
+                    stage_far(c - 1)
+                if c >= 2:
+                    stage_late(c - 2)
+                if c >= 3:
+                    stage_out(c - 3)
         stage_near(c)
+    stage_late(last - 2)
     stage_far(last - 1)
+    stage_out(last - 3)
     stage_out(last - 2)
     stage_late(last - 1)
     stage_out(last - 1)
@@ -429,9 +460,9 @@
                         pltpu.VMEM((full, 2, 3, tok // 2, blk), F32), pltpu.VMEM((2, 3, tok // 2, rest), F32),
                         dma((slots,)), dma((local_exp,)),
                         dma((last,)), dma((last,)), dma((last, 2, 2)), dma((last, 2, 2)), dma((last, 2)), dma((last, 2))],
-        compiler_params=pltpu.CompilerParams(collective_id=1, has_side_effects=True, vmem_limit_bytes=VMEM_LIMIT),
+        compiler_params=pltpu.CompilerParams(collective_id=1, has_side_effects=True, vmem_limit_bytes=DOWN_VMEM),
         name='down',
-    )(z, pos, p, x, b, w)
+    )(in_vmem(z), in_vmem(pos), in_vmem(p), x, b, w)
 
 
 def solution(mesh):
@@ -445,8 +476,9 @@
         experts = local_exp * n
         max_rows = n * (4 * top_k * tok // experts)
         blk = 768 if w_gate_up.shape[2] >= 2048 else 256
-        hall, pos, post, p = dispatch(x_in, expert_ids.T, norm_weight, router_w.T, router_b, n, local_exp)
-        z = gate_up(hall, post, w_gate_up, b_gate_up, max_rows, blk, min(128, max_rows), 4)
+        npre = min(7, w_gate_up.shape[2] // blk)
+        hall, pos, post, p, pre = dispatch(x_in, expert_ids.T, norm_weight, router_w.T, router_b, w_gate_up, n, local_exp, blk, npre)
+        z = gate_up(hall, post, pre, w_gate_up, b_gate_up, max_rows, min(128, max_rows), 3)
         return down(z, pos, p, x_in, w_down, b_down, n, 512 if blk == 768 else 128, 4)
 
     return jax.shard_map(local_block, mesh=mesh, in_specs=(rows_spec, rows_spec, P(), P(), P(), P('ep', None, None), P('ep', None), P('ep', None, None), P('ep', None)), out_specs=rows_spec, check_vma=False)

time: 150 us -> 129 us (0.86); the launches traced: 151 us -> 132 us
  Pallas kernels: 149 us -> 126 us
  local copies, waits for them, and re-layouts: 1.76 us -> 5.7 us
    pallas_call x1, Pallas kernels: 51.6 us -> 39.7 us  [gate_up(): pl.pallas_call(functools.partial(gate_up_kernel, m_blk, slots), out_shape...]
    pallas_call x1, Pallas kernels: 69.4 us -> 61 us  [down(): pl.pallas_call(functools.partial(down_kernel, n, chunks, slots), out_shap...]
    unnamed x1 -> x11, local copies, waits for them, and re-layouts: 1.76 us -> 5.7 us
    pallas_call x1, Pallas kernels: 28.3 us -> 25.5 us  [dispatch(): pl.pallas_call(functools.partial(dispatch_kernel, n, local_exp), out_shap...]
where the time goes in v3:
time: 129 us; the launch traced here: 132 us
  Pallas kernels  126 us (98%)
  local copies, waits for them, and re-layouts  5.7 us (4%)
    pallas_call x1, Pallas kernels, down(): pl.pallas_call(functools.partial(down_kernel, n, chunks, slots), out_shap...  61 us
    pallas_call x1, Pallas kernels, gate_up(): pl.pallas_call(functools.partial(gate_up_kernel, m_blk, slots), out_shape...  39.7 us
    pallas_call x1, Pallas kernels, dispatch(): pl.pallas_call(functools.partial(dispatch_kernel, n, local_exp), out_shap...  25.5 us
    unnamed x11, local copies, waits for them, and re-layouts  5.7 us

profile of v3, /device:TPU:112, one launch (start us, length us, event | category | flops | bytes accessed | tf_op | source)
XLA Modules:
  0.0 131.9 jit_solution(6110654220949078077)
XLA Ops:
  0.0 0.0 copy-start
  0.0 1.0 copy-done
  1.0 0.0 copy-start.1
  1.0 0.9 copy-done.1
  1.9 0.0 copy-start.2
  1.9 0.7 copy-done.2
  2.6 0.0 copy-start.3
  2.6 0.7 copy-done.3
  3.3 0.0 copy-start.4
  3.3 0.7 copy-done.4
  3.9 25.5 %dispatch.1 = (bf16[8,64,2880]{2,1,0:T(8,128)(2,1)S(1)}, f32[512,8]{1,0:T(8,128)S(1)}, f32[8,512]{1,0:T(8,128)S(1)}, f32[512,4]{1,0:T(8,128)S(1)}, bf16[7,2880,768]{2,1,0:T(8,128)(2,1)S(1)}) custom-call(bf16[64,2880]{1,0:T(8,128)(2,1)S(1)} %copy-done, s32[4,64]{1,0:T(4,128)S(1)} %bitcast.3, bf16[2880]{0:T(1024)(128)(2,1)S(1)} %copy-done.2, ...), custom_call_target="tpu_custom_call" | custom-call | tf_op jit(solution)/shard_map/dispatch/pallas_call | solution.py:161
  29.4 39.7 %gate_up.1.z_ref = bf16[4,256,2880]{2,1,0:T(8,128)(2,1)S(1)} custom-call(bf16[8,64,2880]{2,1,0:T(8,128)(2,1)S(1)} %get-tuple-element.10.hall, f32[8,512]{1,0:T(8,128)S(1)} %get-tuple-element.11.post_ref, bf16[7,2880,768]{2,1,0:T(8,128)(2,1)S(1)} %get-tuple-element.12.pre, bf16[4,5760]{1,0:T(4,128)(2,1)} %b_ref.2, bf16[4,2880,5760]{2,1,0:T(8,128)(2,1)} %w_hbm.4), custom_call_target="tpu_custom_call" | custom-call | tf_op jit(solution)/shard_map/gate_up/pallas_call | solution.py:292
  69.1 61.0 %down.1 = bf16[64,2880]{1,0:T(8,128)(2,1)} custom-call(bf16[4,256,2880]{2,1,0:T(8,128)(2,1)S(1)} %gate_up.1.z_ref, f32[512,8]{1,0:T(8,128)S(1)} %get-tuple-element.13.pos_ref, f32[512,4]{1,0:T(8,128)S(1)} %get-tuple-element.14.p_ref, bf16[64,2880]{1,0:T(8,128)(2,1)} %x_ref.3, bf16[4,2880]{1,0:T(4,128)(2,1)} %b_ref.3, bf16[4,2880,2880]{2,1,0:T(8,128)(2,1)} %w_hbm.5), custom_call_target="tpu_custom_call" | custom-call | tf_op jit(solution)/shard_map/down/pallas_call | solution.py:451
  130.1 1.8 %copy.11 = bf16[64,2880]{1,0:T(8,128)(2,1)} copy(bf16[64,2880]{1,0:T(8,128)(2,1)} %down.1) | data formatting | bytes 737280
Async XLA Ops:
  0.0 1.0 copy-start
  1.0 0.9 copy-start.1
  1.9 0.7 copy-start.2
  2.6 0.7 copy-start.3
  3.3 0.7 copy-start.4

commit v4 on v3

--- a/solution.py
+++ b/solution.py
@@ -13,7 +13,7 @@
 F32 = jnp.float32
 BF16 = jnp.bfloat16
 DISPATCH_VMEM = 10 * 1024 * 1024
-GATE_UP_VMEM = 20 * 1024 * 1024
+GATE_UP_VMEM = 22 * 1024 * 1024
 DOWN_VMEM = 48 * 1024 * 1024
 
 
@@ -25,12 +25,20 @@
     return pltpu.with_memory_space_constraint(a, pltpu.VMEM)
 
 
+def vmem_out(shape, dtype):
+    return pltpu.VMEM(shape, dtype)
+
+
+def in_hbm(a):
+    return pltpu.with_memory_space_constraint(a, pltpu.HBM)
+
+
 def dot_t(a, b):
     return lax.dot_general(a, b, (((0,), (0,)), ((), ())), preferred_element_type=F32)
 
 
-def dispatch_kernel(n, local_exp, x_ref, ids_ref, g_ref, wr_ref, br_ref, w_hbm, hall, pos_ref, post_ref, p_ref, pre,
-                    mall, psem, sa, ra, sb, rb, sc, rc, sd, rd, sm, rm):
+def dispatch_kernel(n, local_exp, x_hbm, ids_hbm, g_hbm, wr_hbm, br_hbm, w_hbm, hall, pos_ref, post_ref, p_ref, pre,
+                    x_ref, ids_ref, g_ref, wr_ref, br_ref, isem, mall, psem, sa, ra, sb, rb, sc, rc, sd, rd, sm, rm):
     me = lax.axis_index('ep')
     chips = n // 2
     chip, core = me // 2, me % 2
@@ -48,11 +56,17 @@
 
     half = tok // 2
 
+    loads = [pltpu.make_async_copy(src, dst, isem.at[i]) for i, (src, dst) in enumerate(
+        ((x_hbm, x_ref), (g_hbm, g_ref), (wr_hbm, wr_ref), (br_hbm, br_ref), (ids_hbm, ids_ref)))]
+    for c in loads:
+        c.start()
     barrier = pltpu.get_barrier_semaphore()
     for k in range(1, n):
         pl.semaphore_signal(barrier, inc=1, device_id={'ep': (me + k) % n}, device_id_type=pl.DeviceIdType.MESH)
     blk = pre.shape[2]
     ahead = [pltpu.make_async_copy(w_hbm.at[0, :, pl.ds(j * blk, blk)], pre.at[j], psem.at[j]) for j in range(pre.shape[0])]
+    for c in loads:
+        c.wait()
     for c in ahead:
         c.start()
 
@@ -157,23 +171,27 @@
     tok, d_model = x.shape
     tokens = n * tok
     vm = pl.BlockSpec(memory_space=pltpu.VMEM)
+    hbm = pl.BlockSpec(memory_space=pltpu.HBM)
     dma = pltpu.SemaphoreType.DMA
     hall, pos, post, p, pre = pl.pallas_call(
         functools.partial(dispatch_kernel, n, local_exp),
-        out_shape=(pltpu.VMEM((n, tok, d_model), BF16), pltpu.VMEM((tokens, 8), F32), pltpu.VMEM((8, tokens), F32),
-                   pltpu.VMEM((tokens, local_exp), F32), pltpu.VMEM((npre, d_model, blk), BF16)),
-        in_specs=[vm] * 5 + [pl.BlockSpec(memory_space=pl.ANY)],
+        out_shape=(vmem_out((n, tok, d_model), BF16), vmem_out((tokens, 8), F32), vmem_out((8, tokens), F32),
+                   vmem_out((tokens, local_exp), F32), vmem_out((npre, d_model, blk), BF16)),
+        in_specs=[hbm] * 6,
         out_specs=(vm,) * 5,
-        scratch_shapes=[pltpu.VMEM((n, 2, tok, wr.shape[0]), F32), dma((npre,)),
+        scratch_shapes=[pltpu.VMEM(x.shape, x.dtype), pltpu.VMEM(ids.shape, ids.dtype), pltpu.VMEM(g.shape, g.dtype),
+                        pltpu.VMEM(wr.shape, wr.dtype), pltpu.VMEM(br.shape, br.dtype), dma((5,)),
+                        pltpu.VMEM((n, 2, tok, wr.shape[0]), F32), dma((npre,)),
                         dma, dma, dma((2, 2)), dma((2, 2)), dma((2,)), dma((2,)), dma((2, 3)), dma((2, 3)),
                         dma((n - 1,)), dma((n - 1,))],
         compiler_params=pltpu.CompilerParams(collective_id=0, has_side_effects=True, vmem_limit_bytes=DISPATCH_VMEM),
         name='dispatch',
-    )(x, ids, g, wr, br, w)
+    )(in_hbm(x), in_hbm(ids), in_hbm(g), in_hbm(wr), in_hbm(br), w)
     return hall, pos, post, p, pre
 
 
-def gate_up_kernel(m_blk, slots, hall, post_ref, pre, b_ref, w_hbm, z_ref, wbuf, xg, perm, bias_ref, sems):
+def gate_up_kernel(m_blk, slots, hall, post_ref, pre, b_ref, w_hbm, z_ref,
+                   wbuf, xg, ubuf, perm, bias_ref, sems):
     local_exp, d_model, width = w_hbm.shape
     npre, _, blk = pre.shape
     full, rest = width // blk, width % blk
@@ -225,25 +243,30 @@
         lax.fori_loop(0, chunks, body, 0)
         return chunks
 
+    def glu(e, j, m, cols):
+        at = pl.ds(pl.multiple_of(m * m_blk, m_blk), m_blk)
+        for t in range(0, cols, 256):
+            wide = min(256, cols - t)
+            if wide == 256:
+                pm = perm[...]
+            else:
+                pm = jnp.concatenate([perm[:128, :64], perm[:128, 128:192]], axis=1)
+            al = dot32(ubuf[m, :, t:t + wide], pm)
+            gate = jnp.minimum(al[:, :wide // 2], LIMIT)
+            linear = jnp.clip(al[:, wide // 2:], -LIMIT, LIMIT)
+            z = gate * jax.nn.sigmoid(ALPHA * gate) * (linear + 1.0)
+            zoff = pl.multiple_of(j * (blk // 2), 128) + t // 2
+            z_ref[e, at, pl.ds(zoff, wide // 2)] = z.astype(BF16)
+
     def compute(e, j, cols, chunks, weights):
         off = pl.multiple_of(j * blk, 128)
         bias = bias_ref[pl.ds(e, 1), pl.ds(off, cols)]
+        before = j - 1 if isinstance(j, int) else jnp.maximum(j - 1, 0)
 
         def rows(m, c):
             at = pl.ds(pl.multiple_of(m * m_blk, m_blk), m_blk)
-            u = (dot32(xg[at, :], weights()) + bias).astype(BF16)
-            for t in range(0, cols, 256):
-                wide = min(256, cols - t)
-                if wide == 256:
-                    pm = perm[...]
-                else:
-                    pm = jnp.concatenate([perm[:128, :64], perm[:128, 128:192]], axis=1)
-                al = dot32(u[:, t:t + wide], pm)
-                gate = jnp.minimum(al[:, :wide // 2], LIMIT)
-                linear = jnp.clip(al[:, wide // 2:], -LIMIT, LIMIT)
-                z = gate * jax.nn.sigmoid(ALPHA * gate) * (linear + 1.0)
-                zoff = pl.multiple_of(j * (blk // 2), 128) + t // 2
-                z_ref[e, at, pl.ds(zoff, wide // 2)] = z.astype(BF16)
+            glu(e, before, m, blk)
+            ubuf[m, :, :cols] = (dot32(xg[at, :], weights()) + bias).astype(BF16)
             return c
 
         lax.fori_loop(0, chunks, rows, 0)
@@ -273,8 +296,13 @@
         if first:
             lax.fori_loop(0, npre, from_pre, 0)
         lax.fori_loop(npre if first else 0, full, body, 0)
-        if rest:
-            streamed(e, jnp.int32(full), rest, chunks)
+        streamed(e, full, rest, chunks)
+
+        def end(m, c):
+            glu(e, full, m, rest)
+            return c
+
+        lax.fori_loop(0, chunks, end, 0)
 
     expert(0, True)
 
@@ -289,12 +317,14 @@
     local_exp, d_model, width = w.shape
     blk = pre.shape[2]
     vm = pl.BlockSpec(memory_space=pltpu.VMEM)
+    hbm = pl.BlockSpec(memory_space=pl.ANY)
     return pl.pallas_call(
         functools.partial(gate_up_kernel, m_blk, slots),
-        out_shape=pltpu.VMEM((local_exp, max_rows, width // 2), BF16),
-        in_specs=[vm, vm, vm, vm, pl.BlockSpec(memory_space=pl.ANY)],
+        out_shape=vmem_out((local_exp, max_rows, width // 2), BF16),
+        in_specs=[vm, vm, vm, vm, hbm],
         out_specs=vm,
         scratch_shapes=[pltpu.VMEM((slots, d_model, blk), BF16), pltpu.VMEM((max_rows, d_model), BF16),
+                        pltpu.VMEM((max_rows // m_blk, m_blk, blk), BF16),
                         pltpu.VMEM((256, 256), BF16), pltpu.VMEM((local_exp, width), F32), pltpu.SemaphoreType.DMA((slots,))],
         compiler_params=pltpu.CompilerParams(vmem_limit_bytes=GATE_UP_VMEM),
         name='gate_up',
@@ -329,7 +359,10 @@
         src = w_hbm.at[q % local_exp, :, pl.ds(off, cols)]
         if cols == blk:
             return pltpu.make_async_copy(src, wbuf.at[q % slots], wsem.at[q % slots])
-        return pltpu.make_async_copy(src, wrest.at[q % local_exp], rsem.at[q % local_exp])
+        return pltpu.make_async_copy(src, wrest.at[q % slots], rsem.at[q % slots])
+
+    def weights(q, cols):
+        return wbuf[q % slots] if cols == blk else wrest[q % slots]
 
     for q in range(depth):
         block_copy(q).start()
@@ -411,8 +444,7 @@
             if q + depth < total:
                 block_copy(q + depth).start()
             block_copy(q).wait()
-            wv = wbuf[q % slots] if cols == blk else wrest[e]
-            y = dot32(z_ref[e], wv) + bias[e:e + 1, off:off + cols]
+            y = dot32(z_ref[e], weights(q, cols)) + bias[e:e + 1, off:off + cols]
             y = jnp.where(row_ids < counts[e], y, 0.0).astype(BF16)
             add = (p_ref[:, e:e + 1] * dot32(scat[e], y)).reshape(2, nchip, tok, cols)
             if e == 0:
@@ -422,6 +454,7 @@
             if e == 1:
                 if c >= 1:
                     stage_far(c - 1)
+            if e == 2:
                 if c >= 2:
                     stage_late(c - 2)
                 if c >= 3:
@@ -453,12 +486,12 @@
         out_shape=jax.ShapeDtypeStruct((tok, width), BF16),
         in_specs=[vm, vm, vm, vm, vm, pl.BlockSpec(memory_space=pl.ANY)],
         out_specs=vm,
-        scratch_shapes=[pltpu.VMEM((slots, d_ff, blk), BF16), pltpu.VMEM((local_exp, d_ff, rest), BF16),
+        scratch_shapes=[pltpu.VMEM((slots, d_ff, blk), BF16), pltpu.VMEM((slots, d_ff, rest), BF16),
                         pltpu.VMEM((local_exp, tokens, z.shape[1]), BF16),
                         pltpu.VMEM((full, 2, n // 2, tok, blk), F32), pltpu.VMEM((2, n // 2, tok, rest), F32),
                         pltpu.VMEM((full, n // 2, tok, blk), F32), pltpu.VMEM((n // 2, tok, rest), F32),
                         pltpu.VMEM((full, 2, 3, tok // 2, blk), F32), pltpu.VMEM((2, 3, tok // 2, rest), F32),
-                        dma((slots,)), dma((local_exp,)),
+                        dma((slots,)), dma((slots,)),
                         dma((last,)), dma((last,)), dma((last, 2, 2)), dma((last, 2, 2)), dma((last, 2)), dma((last, 2))],
         compiler_params=pltpu.CompilerParams(collective_id=1, has_side_effects=True, vmem_limit_bytes=DOWN_VMEM),
         name='down',
@@ -475,10 +508,11 @@
         local_exp = w_gate_up.shape[0]
         experts = local_exp * n
         max_rows = n * (4 * top_k * tok // experts)
-        blk = 768 if w_gate_up.shape[2] >= 2048 else 256
-        npre = min(7, w_gate_up.shape[2] // blk)
+        wide = w_gate_up.shape[2] >= 2048
+        blk, dcol = (1024, 512) if wide else (256, 128)
+        npre = w_gate_up.shape[2] // blk
         hall, pos, post, p, pre = dispatch(x_in, expert_ids.T, norm_weight, router_w.T, router_b, w_gate_up, n, local_exp, blk, npre)
         z = gate_up(hall, post, pre, w_gate_up, b_gate_up, max_rows, min(128, max_rows), 3)
-        return down(z, pos, p, x_in, w_down, b_down, n, 512 if blk == 768 else 128, 4)
+        return down(z, pos, p, x_in, w_down, b_down, n, dcol, 4)
 
     return jax.shard_map(local_block, mesh=mesh, in_specs=(rows_spec, rows_spec, P(), P(), P(), P('ep', None, None), P('ep', None), P('ep', None, None), P('ep', None)), out_specs=rows_spec, check_vma=False)

time: 129 us -> 121 us (0.938); the launches traced: 132 us -> 122 us
  Pallas kernels: 126 us -> 120 us
  local copies, waits for them, and re-layouts: 5.7 us -> 1.76 us
    unnamed x11 -> x1, local copies, waits for them, and re-layouts: 5.7 us -> 1.76 us
    pallas_call x1, Pallas kernels: 61 us -> 57.4 us  [down(): pl.pallas_call(functools.partial(down_kernel, n, chunks, slots), out_shap...]
    pallas_call x1, Pallas kernels: 39.7 us -> 36.9 us  [gate_up(): pl.pallas_call(functools.partial(gate_up_kernel, m_blk, slots), out_shape...]
where the time goes in v4:
time: 121 us; the launch traced here: 122 us
  Pallas kernels  120 us (99%)
  local copies, waits for them, and re-layouts  1.76 us (1%)
    pallas_call x1, Pallas kernels, down(): pl.pallas_call(functools.partial(down_kernel, n, chunks, slots), out_shap...  57.4 us
    pallas_call x1, Pallas kernels, gate_up(): pl.pallas_call(functools.partial(gate_up_kernel, m_blk, slots), out_shape...  36.9 us
    pallas_call x1, Pallas kernels, dispatch(): pl.pallas_call(functools.partial(dispatch_kernel, n, local_exp), out_shap...  25.8 us

profile of v4, /device:TPU:112, one launch (start us, length us, event | category | flops | bytes accessed | tf_op | source)
XLA Modules:
  0.0 121.9 jit_solution(8477703602373964578)
XLA Ops:
  0.0 25.8 %dispatch.1 = (bf16[8,64,2880]{2,1,0:T(8,128)(2,1)S(1)}, f32[512,8]{1,0:T(8,128)S(1)}, f32[8,512]{1,0:T(8,128)S(1)}, f32[512,4]{1,0:T(8,128)S(1)}, bf16[5,2880,1024]{2,1,0:T(8,128)(2,1)S(1)}) custom-call(bf16[64,2880]{1,0:T(8,128)(2,1)} %x_ref.1, s32[4,64]{1,0:T(4,128)} %bitcast.3, bf16[2880]{0:T(1024)(128)(2,1)} %g_hbm.1, bf16[32,2880]{1,0:T(8,128)(2,1)} %bitcast.2, ...), custom_call_target="tpu_custom_call" | custom-call | tf_op jit(solution)/shard_map/dispatch/pallas_call | solution.py:176
  25.8 36.9 %gate_up.1.z_ref = bf16[4,256,2880]{2,1,0:T(8,128)(2,1)S(1)} custom-call(bf16[8,64,2880]{2,1,0:T(8,128)(2,1)S(1)} %get-tuple-element.10.hall, f32[8,512]{1,0:T(8,128)S(1)} %get-tuple-element.11.post_ref, bf16[5,2880,1024]{2,1,0:T(8,128)(2,1)S(1)} %get-tuple-element.12.pre, bf16[4,5760]{1,0:T(4,128)(2,1)} %b_ref.2, bf16[4,2880,5760]{2,1,0:T(8,128)(2,1)} %w_hbm.4), custom_call_target="tpu_custom_call" | custom-call | tf_op jit(solution)/shard_map/gate_up/pallas_call | solution.py:321
  62.8 57.4 %down.1 = bf16[64,2880]{1,0:T(8,128)(2,1)} custom-call(bf16[4,256,2880]{2,1,0:T(8,128)(2,1)S(1)} %gate_up.1.z_ref, f32[512,8]{1,0:T(8,128)S(1)} %get-tuple-element.13.pos_ref, f32[512,4]{1,0:T(8,128)S(1)} %get-tuple-element.14.p_ref, bf16[64,2880]{1,0:T(8,128)(2,1)} %x_ref.1, bf16[4,2880]{1,0:T(4,128)(2,1)} %b_ref.3, bf16[4,2880,2880]{2,1,0:T(8,128)(2,1)} %w_hbm.5), custom_call_target="tpu_custom_call" | custom-call | tf_op jit(solution)/shard_map/down/pallas_call | solution.py:484
  120.2 1.8 %copy.11 = bf16[64,2880]{1,0:T(8,128)(2,1)} copy(bf16[64,2880]{1,0:T(8,128)(2,1)} %down.1) | data formatting | bytes 737280
